TPU v7x, 32 devices: a whole 2x2x4 slice. The times are simulated.
32 devices in a mesh: layer: 8 (over z, x), plane: 4 (over y, core).
Axes of the slice: x: 2, y: 2, z: 4, core: 2. Of those that a mesh axis runs over, the one named last changes fastest.
Arguments:
- sources: float32 [8, 16, 4096], P('layer', None, 'plane'), may hold values from -6 to 6
- fronts: float32 [8, 32, 128, 128], P('layer', 'plane'), as said below
- down_left: bfloat16 [8, 4, 128, 4096], P('layer', None, None, 'plane'), may hold values from -0.1875 to 0.1875
- down_right: bfloat16 [8, 4, 128, 4096], P('layer', None, None, 'plane'), may hold values from -0.4375 to 0.4375
- up_left: bfloat16 [8, 4, 128, 4096], P('layer', None, None, 'plane'), may hold values from -0.1875 to 0.1875
- up_right: bfloat16 [8, 4, 128, 4096], P('layer', None, None, 'plane'), may hold values from -0.4375 to 0.4375
- ranks: int32 [8, 2, 4, 4], P('layer', None, 'plane'), may hold values from 1 to 128
- pattern: int32 [8, 2, 4, 4], P('layer', None, 'plane'), may hold values 0 or 1
Outputs:
- field: float32 [8, 16, 4096], P('layer', None, 'plane')
Inputs may be any that keep to these rules, and one draw needn't show every extreme that they name: fronts[l, b] is lower triangular with every diagonal entry between 1 and 4.
All inputs are finite; a program needn't handle non-finite values. No bound on the sum of `pattern` on one device may be relied on, other than what follows from the above.
Results may differ from a plain program's by a relative error of at most 0.025.
Values may be sent and summed in bfloat16 or wider, within the bound.
No kernel may reach another device: no remote copies, remote signals or barrier semaphores. Data moves between devices by JAX's collectives and lax.ppermute only.
A program may use at most 64 MiB of HBM per device.

v0:
```python
import jax
import jax.numpy as jnp
from jax import lax
from jax.sharding import PartitionSpec as P


def shifted(value, axis, by):
    length = lax.axis_size(axis)
    pairs = [(i, i + by) for i in range(length) if 0 <= i + by < length]
    return lax.ppermute(value, axis, pairs)


def front_solve(source, front_blocks):
    stacked = source.reshape(
        source.shape[0], front_blocks.shape[0], front_blocks.shape[1]
    ).transpose(1, 2, 0)
    solved = jax.scipy.linalg.solve_triangular(front_blocks, stacked, lower=True)
    return solved.transpose(2, 0, 1).reshape(source.shape)


def compress(trace, factor_in):
    return jnp.einsum(
        "ikt,st->isk", factor_in, trace.astype(jnp.bfloat16), preferred_element_type=jnp.float32
    ).astype(jnp.bfloat16)


def expand(coeffs, factor_out, keep_mask):
    return jnp.einsum(
        "jsk,jkt->st",
        coeffs * keep_mask[:, None, :],
        factor_out,
        preferred_element_type=jnp.float32,
    )


def shards(sources, fronts, down_left, down_right, up_left, up_right, ranks, pattern):
    solved = front_solve(sources[0], fronts[0])
    layer_count = lax.axis_size("layer")
    layer_at = lax.axis_index("layer")
    group_count = 1
    group_rows = solved.shape[0] // group_count
    total_turns = layer_count + group_count - 1
    rank_top = down_left.shape[2]
    ladder = jnp.arange(rank_top, dtype=jnp.int32)
    keep_mask = (
        pattern[0, :, 0, :, None]
        * (ladder[None, None, :] < ranks[0, :, 0, :, None]).astype(jnp.int32)
    ).astype(jnp.bfloat16)
    down_factor = down_left[0]
    up_factor = up_left[0]

    def advance(step_at, carry):
        down_last, up_last, down_all, up_all = carry
        down_in = shifted(down_last.astype(jnp.bfloat16), "layer", 1).astype(down_last.dtype)
        up_in = shifted(up_last.astype(jnp.bfloat16), "layer", -1).astype(up_last.dtype)
        down_coeffs = compress(down_in, down_factor)
        up_coeffs = compress(up_in, up_factor)
        down_group = step_at - layer_at
        up_group = step_at - (layer_count - 1 - layer_at)
        down_start = jnp.clip(down_group, 0, group_count - 1) * group_rows
        up_start = jnp.clip(up_group, 0, group_count - 1) * group_rows
        arrived = (
            lax.all_to_all(down_coeffs, "plane", split_axis=0, concat_axis=0, tiled=True),
            lax.all_to_all(up_coeffs, "plane", split_axis=0, concat_axis=0, tiled=True),
        )
        down_new = solved + expand(arrived[0], down_right[0], keep_mask[0])
        up_new = solved + expand(arrived[1], up_right[0], keep_mask[1])
        down_valid = (down_group >= 0) & (down_group < group_count)
        up_valid = (up_group >= 0) & (up_group < group_count)
        down_all = jnp.where(down_valid, down_new, down_all)
        up_all = jnp.where(up_valid, up_new, up_all)
        return (down_new, up_new, down_all, up_all)

    empty_group = jnp.zeros((group_rows, solved.shape[1]), jnp.float32)
    empty_all = jnp.zeros(solved.shape, jnp.float32)
    _, _, down_all, up_all = lax.fori_loop(
        0, total_turns, advance, (empty_group, empty_group, empty_all, empty_all)
    )
    field = down_all + up_all - solved
    return field[None]


def solution(mesh):
    in_specs = (
        P("layer", None, "plane"),
        P("layer", "plane", None, None),
        P("layer", None, None, "plane"),
        P("layer", None, None, "plane"),
        P("layer", None, None, "plane"),
        P("layer", None, None, "plane"),
        P("layer", None, "plane", None),
        P("layer", None, "plane", None),
    )
    out_specs = P("layer", None, "plane")
    return jax.shard_map(shards, mesh=mesh, in_specs=in_specs, out_specs=out_specs, check_vma=False)
```

profile of v0, /device:TPU:0, one launch (start us, length us, event | category | flops | bytes accessed | tf_op | source)
XLA Modules:
  0.0 272.3 jit_solution(13083170746094652693)
XLA Ops:
  1.2 78.6 %custom-call.4 = f32[8,1,128,128]{2,3,1,0:T(8,128)S(1)} custom-call(f32[8,1,128,128]{3,2,1,0:T(8,128)S(1)} %select_bitcast_fusion), custom_call_target="InvertDiagBlocksLowerTriangular" | custom-call | tf_op jit(solution)/shard_map/jit(_solve_triangular)/vmap()/triangular_solve | solution.py:17
  82.0 189.6 %while.21 = (s32[]{:T(128)}, bf16[16,1024]{1,0:T(8,128)(2,1)S(1)}, bf16[16,1024]{1,0:T(8,128)(2,1)S(1)}, f32[16,1024]{1,0:T(8,128)S(1)}, f32[16,1024]{1,0:T(8,12...) while((s32[]{:T(128)}, bf16[16,1024]{1,0:T(8,128)(2,1)S(1)}, ...), condition=%wide.region_1.2_spmd.clone, body=%wide.region_0.1_spmd.clone.sunk | while | flops 67305480 | bytes 13670822 | solution.py:76
  83.5 5.5 %collective-permute-start = (bf16[16,1024]{1,0:T(8,128)(2,1)S(1)}, bf16[16,1024]{1,0:T(8,128)(2,1)S(1)}, u32[]{:S(2)}, u32[]{:S(2)}) collective-permute-start(bf16[16,1024]{1,0:T(8,128)(2,1)S(1)} %select_convert_fusion.5), channel_id=1, source_target_pairs={{0,4},{4,8},{8,12},{12,16},{16,20},{20,24},{24,28},{1,5},{5,9},{9,... | collective-permute-start | bytes 98312 | tf_op jit(solution)/shard_map/while/body/eval_jaxpr/ppermute | solution.py:10
  89.1 2.3 fusion.28
  91.4 3.3 %all-to-all-start.1 = ((bf16[4,16,128]{2,1,0:T(8,128)(2,1)}), bf16[4,16,128]{2,1,0:T(8,128)(2,1)S(1)}, u32[]{:S(2)}, u32[]{:S(2)}) async-start(bf16[4,16,128]{2,1,0:T(8,128)(2,1)} %fusion.28), calls=%async_computation.1 | async-start | bytes 32768 | tf_op jit(solution)/shard_map/while/body/eval_jaxpr/all_to_all | solution.py:64
  95.7 2.9 %all-to-all-done.1 = bf16[4,16,128]{2,1,0:T(8,128)(2,1)S(1)} async-done(((bf16[4,16,128]{2,1,0:T(8,128)(2,1)}), bf16[4,16,128]{2,1,0:T(8,128)(2,1)S(1)}, u32[]{:S(2)}, u32[]{:S(2)}) %all-to-all-start.1) | async-done | bytes 16416 | tf_op jit(solution)/shard_map/while/body/eval_jaxpr/all_to_all | solution.py:64
  98.6 3.3 %all-to-all-start = ((bf16[4,16,128]{2,1,0:T(8,128)(2,1)}), bf16[4,16,128]{2,1,0:T(8,128)(2,1)S(1)}, u32[]{:S(2)}, u32[]{:S(2)}) async-start(bf16[4,16,128]{2,1,0:T(8,128)(2,1)} %fusion.27), calls=%async_computation | async-start | bytes 32768 | tf_op jit(solution)/shard_map/while/body/eval_jaxpr/all_to_all | solution.py:63
  102.1 3.6 %all-to-all-done = bf16[4,16,128]{2,1,0:T(8,128)(2,1)S(1)} async-done(((bf16[4,16,128]{2,1,0:T(8,128)(2,1)}), bf16[4,16,128]{2,1,0:T(8,128)(2,1)S(1)}, u32[]{:S(2)}, u32[]{:S(2)}) %all-to-all-start) | async-done | bytes 16416 | tf_op jit(solution)/shard_map/while/body/eval_jaxpr/all_to_all | solution.py:63
  107.4 5.4 %collective-permute-start = (bf16[16,1024]{1,0:T(8,128)(2,1)S(1)}, bf16[16,1024]{1,0:T(8,128)(2,1)S(1)}, u32[]{:S(2)}, u32[]{:S(2)}) collective-permute-start(bf16[16,1024]{1,0:T(8,128)(2,1)S(1)} %select_convert_fusion.5), channel_id=1, source_target_pairs={{0,4},{4,8},{8,12},{12,16},{16,20},{20,24},{24,28},{1,5},{5,9},{9,... | collective-permute-start | bytes 98312 | tf_op jit(solution)/shard_map/while/body/eval_jaxpr/ppermute | solution.py:10
  112.8 2.3 fusion.28
  115.1 3.2 %all-to-all-start.1 = ((bf16[4,16,128]{2,1,0:T(8,128)(2,1)}), bf16[4,16,128]{2,1,0:T(8,128)(2,1)S(1)}, u32[]{:S(2)}, u32[]{:S(2)}) async-start(bf16[4,16,128]{2,1,0:T(8,128)(2,1)} %fusion.28), calls=%async_computation.1 | async-start | bytes 32768 | tf_op jit(solution)/shard_map/while/body/eval_jaxpr/all_to_all | solution.py:64
  119.3 2.8 %all-to-all-done.1 = bf16[4,16,128]{2,1,0:T(8,128)(2,1)S(1)} async-done(((bf16[4,16,128]{2,1,0:T(8,128)(2,1)}), bf16[4,16,128]{2,1,0:T(8,128)(2,1)S(1)}, u32[]{:S(2)}, u32[]{:S(2)}) %all-to-all-start.1) | async-done | bytes 16416 | tf_op jit(solution)/shard_map/while/body/eval_jaxpr/all_to_all | solution.py:64
  122.2 3.3 %all-to-all-start = ((bf16[4,16,128]{2,1,0:T(8,128)(2,1)}), bf16[4,16,128]{2,1,0:T(8,128)(2,1)S(1)}, u32[]{:S(2)}, u32[]{:S(2)}) async-start(bf16[4,16,128]{2,1,0:T(8,128)(2,1)} %fusion.27), calls=%async_computation | async-start | bytes 32768 | tf_op jit(solution)/shard_map/while/body/eval_jaxpr/all_to_all | solution.py:63
  125.7 3.6 %all-to-all-done = bf16[4,16,128]{2,1,0:T(8,128)(2,1)S(1)} async-done(((bf16[4,16,128]{2,1,0:T(8,128)(2,1)}), bf16[4,16,128]{2,1,0:T(8,128)(2,1)S(1)}, u32[]{:S(2)}, u32[]{:S(2)}) %all-to-all-start) | async-done | bytes 16416 | tf_op jit(solution)/shard_map/while/body/eval_jaxpr/all_to_all | solution.py:63
  131.0 5.4 %collective-permute-start = (bf16[16,1024]{1,0:T(8,128)(2,1)S(1)}, bf16[16,1024]{1,0:T(8,128)(2,1)S(1)}, u32[]{:S(2)}, u32[]{:S(2)}) collective-permute-start(bf16[16,1024]{1,0:T(8,128)(2,1)S(1)} %select_convert_fusion.5), channel_id=1, source_target_pairs={{0,4},{4,8},{8,12},{12,16},{16,20},{20,24},{24,28},{1,5},{5,9},{9,... | collective-permute-start | bytes 98312 | tf_op jit(solution)/shard_map/while/body/eval_jaxpr/ppermute | solution.py:10
  136.5 2.3 fusion.28
  138.8 3.2 %all-to-all-start.1 = ((bf16[4,16,128]{2,1,0:T(8,128)(2,1)}), bf16[4,16,128]{2,1,0:T(8,128)(2,1)S(1)}, u32[]{:S(2)}, u32[]{:S(2)}) async-start(bf16[4,16,128]{2,1,0:T(8,128)(2,1)} %fusion.28), calls=%async_computation.1 | async-start | bytes 32768 | tf_op jit(solution)/shard_map/while/body/eval_jaxpr/all_to_all | solution.py:64
  143.0 2.8 %all-to-all-done.1 = bf16[4,16,128]{2,1,0:T(8,128)(2,1)S(1)} async-done(((bf16[4,16,128]{2,1,0:T(8,128)(2,1)}), bf16[4,16,128]{2,1,0:T(8,128)(2,1)S(1)}, u32[]{:S(2)}, u32[]{:S(2)}) %all-to-all-start.1) | async-done | bytes 16416 | tf_op jit(solution)/shard_map/while/body/eval_jaxpr/all_to_all | solution.py:64
  145.8 3.3 %all-to-all-start = ((bf16[4,16,128]{2,1,0:T(8,128)(2,1)}), bf16[4,16,128]{2,1,0:T(8,128)(2,1)S(1)}, u32[]{:S(2)}, u32[]{:S(2)}) async-start(bf16[4,16,128]{2,1,0:T(8,128)(2,1)} %fusion.27), calls=%async_computation | async-start | bytes 32768 | tf_op jit(solution)/shard_map/while/body/eval_jaxpr/all_to_all | solution.py:63
  149.4 3.6 %all-to-all-done = bf16[4,16,128]{2,1,0:T(8,128)(2,1)S(1)} async-done(((bf16[4,16,128]{2,1,0:T(8,128)(2,1)}), bf16[4,16,128]{2,1,0:T(8,128)(2,1)S(1)}, u32[]{:S(2)}, u32[]{:S(2)}) %all-to-all-start) | async-done | bytes 16416 | tf_op jit(solution)/shard_map/while/body/eval_jaxpr/all_to_all | solution.py:63
  154.6 5.4 %collective-permute-start = (bf16[16,1024]{1,0:T(8,128)(2,1)S(1)}, bf16[16,1024]{1,0:T(8,128)(2,1)S(1)}, u32[]{:S(2)}, u32[]{:S(2)}) collective-permute-start(bf16[16,1024]{1,0:T(8,128)(2,1)S(1)} %select_convert_fusion.5), channel_id=1, source_target_pairs={{0,4},{4,8},{8,12},{12,16},{16,20},{20,24},{24,28},{1,5},{5,9},{9,... | collective-permute-start | bytes 98312 | tf_op jit(solution)/shard_map/while/body/eval_jaxpr/ppermute | solution.py:10
  160.2 2.3 fusion.28
  162.5 3.2 %all-to-all-start.1 = ((bf16[4,16,128]{2,1,0:T(8,128)(2,1)}), bf16[4,16,128]{2,1,0:T(8,128)(2,1)S(1)}, u32[]{:S(2)}, u32[]{:S(2)}) async-start(bf16[4,16,128]{2,1,0:T(8,128)(2,1)} %fusion.28), calls=%async_computation.1 | async-start | bytes 32768 | tf_op jit(solution)/shard_map/while/body/eval_jaxpr/all_to_all | solution.py:64
  166.7 2.8 %all-to-all-done.1 = bf16[4,16,128]{2,1,0:T(8,128)(2,1)S(1)} async-done(((bf16[4,16,128]{2,1,0:T(8,128)(2,1)}), bf16[4,16,128]{2,1,0:T(8,128)(2,1)S(1)}, u32[]{:S(2)}, u32[]{:S(2)}) %all-to-all-start.1) | async-done | bytes 16416 | tf_op jit(solution)/shard_map/while/body/eval_jaxpr/all_to_all | solution.py:64
  169.5 3.3 %all-to-all-start = ((bf16[4,16,128]{2,1,0:T(8,128)(2,1)}), bf16[4,16,128]{2,1,0:T(8,128)(2,1)S(1)}, u32[]{:S(2)}, u32[]{:S(2)}) async-start(bf16[4,16,128]{2,1,0:T(8,128)(2,1)} %fusion.27), calls=%async_computation | async-start | bytes 32768 | tf_op jit(solution)/shard_map/while/body/eval_jaxpr/all_to_all | solution.py:63
  173.1 3.6 %all-to-all-done = bf16[4,16,128]{2,1,0:T(8,128)(2,1)S(1)} async-done(((bf16[4,16,128]{2,1,0:T(8,128)(2,1)}), bf16[4,16,128]{2,1,0:T(8,128)(2,1)S(1)}, u32[]{:S(2)}, u32[]{:S(2)}) %all-to-all-start) | async-done | bytes 16416 | tf_op jit(solution)/shard_map/while/body/eval_jaxpr/all_to_all | solution.py:63
  178.3 5.4 %collective-permute-start = (bf16[16,1024]{1,0:T(8,128)(2,1)S(1)}, bf16[16,1024]{1,0:T(8,128)(2,1)S(1)}, u32[]{:S(2)}, u32[]{:S(2)}) collective-permute-start(bf16[16,1024]{1,0:T(8,128)(2,1)S(1)} %select_convert_fusion.5), channel_id=1, source_target_pairs={{0,4},{4,8},{8,12},{12,16},{16,20},{20,24},{24,28},{1,5},{5,9},{9,... | collective-permute-start | bytes 98312 | tf_op jit(solution)/shard_map/while/body/eval_jaxpr/ppermute | solution.py:10
  183.8 2.3 fusion.28
  186.2 3.2 %all-to-all-start.1 = ((bf16[4,16,128]{2,1,0:T(8,128)(2,1)}), bf16[4,16,128]{2,1,0:T(8,128)(2,1)S(1)}, u32[]{:S(2)}, u32[]{:S(2)}) async-start(bf16[4,16,128]{2,1,0:T(8,128)(2,1)} %fusion.28), calls=%async_computation.1 | async-start | bytes 32768 | tf_op jit(solution)/shard_map/while/body/eval_jaxpr/all_to_all | solution.py:64
  190.4 2.8 %all-to-all-done.1 = bf16[4,16,128]{2,1,0:T(8,128)(2,1)S(1)} async-done(((bf16[4,16,128]{2,1,0:T(8,128)(2,1)}), bf16[4,16,128]{2,1,0:T(8,128)(2,1)S(1)}, u32[]{:S(2)}, u32[]{:S(2)}) %all-to-all-start.1) | async-done | bytes 16416 | tf_op jit(solution)/shard_map/while/body/eval_jaxpr/all_to_all | solution.py:64
  193.2 3.3 %all-to-all-start = ((bf16[4,16,128]{2,1,0:T(8,128)(2,1)}), bf16[4,16,128]{2,1,0:T(8,128)(2,1)S(1)}, u32[]{:S(2)}, u32[]{:S(2)}) async-start(bf16[4,16,128]{2,1,0:T(8,128)(2,1)} %fusion.27), calls=%async_computation | async-start | bytes 32768 | tf_op jit(solution)/shard_map/while/body/eval_jaxpr/all_to_all | solution.py:63
  196.8 3.6 %all-to-all-done = bf16[4,16,128]{2,1,0:T(8,128)(2,1)S(1)} async-done(((bf16[4,16,128]{2,1,0:T(8,128)(2,1)}), bf16[4,16,128]{2,1,0:T(8,128)(2,1)S(1)}, u32[]{:S(2)}, u32[]{:S(2)}) %all-to-all-start) | async-done | bytes 16416 | tf_op jit(solution)/shard_map/while/body/eval_jaxpr/all_to_all | solution.py:63
  202.0 5.4 %collective-permute-start = (bf16[16,1024]{1,0:T(8,128)(2,1)S(1)}, bf16[16,1024]{1,0:T(8,128)(2,1)S(1)}, u32[]{:S(2)}, u32[]{:S(2)}) collective-permute-start(bf16[16,1024]{1,0:T(8,128)(2,1)S(1)} %select_convert_fusion.5), channel_id=1, source_target_pairs={{0,4},{4,8},{8,12},{12,16},{16,20},{20,24},{24,28},{1,5},{5,9},{9,... | collective-permute-start | bytes 98312 | tf_op jit(solution)/shard_map/while/body/eval_jaxpr/ppermute | solution.py:10
  207.5 2.3 fusion.28
  209.8 3.2 %all-to-all-start.1 = ((bf16[4,16,128]{2,1,0:T(8,128)(2,1)}), bf16[4,16,128]{2,1,0:T(8,128)(2,1)S(1)}, u32[]{:S(2)}, u32[]{:S(2)}) async-start(bf16[4,16,128]{2,1,0:T(8,128)(2,1)} %fusion.28), calls=%async_computation.1 | async-start | bytes 32768 | tf_op jit(solution)/shard_map/while/body/eval_jaxpr/all_to_all | solution.py:64
  214.1 2.8 %all-to-all-done.1 = bf16[4,16,128]{2,1,0:T(8,128)(2,1)S(1)} async-done(((bf16[4,16,128]{2,1,0:T(8,128)(2,1)}), bf16[4,16,128]{2,1,0:T(8,128)(2,1)S(1)}, u32[]{:S(2)}, u32[]{:S(2)}) %all-to-all-start.1) | async-done | bytes 16416 | tf_op jit(solution)/shard_map/while/body/eval_jaxpr/all_to_all | solution.py:64
  216.9 3.3 %all-to-all-start = ((bf16[4,16,128]{2,1,0:T(8,128)(2,1)}), bf16[4,16,128]{2,1,0:T(8,128)(2,1)S(1)}, u32[]{:S(2)}, u32[]{:S(2)}) async-start(bf16[4,16,128]{2,1,0:T(8,128)(2,1)} %fusion.27), calls=%async_computation | async-start | bytes 32768 | tf_op jit(solution)/shard_map/while/body/eval_jaxpr/all_to_all | solution.py:63
  220.4 3.6 %all-to-all-done = bf16[4,16,128]{2,1,0:T(8,128)(2,1)S(1)} async-done(((bf16[4,16,128]{2,1,0:T(8,128)(2,1)}), bf16[4,16,128]{2,1,0:T(8,128)(2,1)S(1)}, u32[]{:S(2)}, u32[]{:S(2)}) %all-to-all-start) | async-done | bytes 16416 | tf_op jit(solution)/shard_map/while/body/eval_jaxpr/all_to_all | solution.py:63
  225.7 5.4 %collective-permute-start = (bf16[16,1024]{1,0:T(8,128)(2,1)S(1)}, bf16[16,1024]{1,0:T(8,128)(2,1)S(1)}, u32[]{:S(2)}, u32[]{:S(2)}) collective-permute-start(bf16[16,1024]{1,0:T(8,128)(2,1)S(1)} %select_convert_fusion.5), channel_id=1, source_target_pairs={{0,4},{4,8},{8,12},{12,16},{16,20},{20,24},{24,28},{1,5},{5,9},{9,... | collective-permute-start | bytes 98312 | tf_op jit(solution)/shard_map/while/body/eval_jaxpr/ppermute | solution.py:10
  233.5 3.2 %all-to-all-start.1 = ((bf16[4,16,128]{2,1,0:T(8,128)(2,1)}), bf16[4,16,128]{2,1,0:T(8,128)(2,1)S(1)}, u32[]{:S(2)}, u32[]{:S(2)}) async-start(bf16[4,16,128]{2,1,0:T(8,128)(2,1)} %fusion.28), calls=%async_computation.1 | async-start | bytes 32768 | tf_op jit(solution)/shard_map/while/body/eval_jaxpr/all_to_all | solution.py:64
  237.8 2.8 %all-to-all-done.1 = bf16[4,16,128]{2,1,0:T(8,128)(2,1)S(1)} async-done(((bf16[4,16,128]{2,1,0:T(8,128)(2,1)}), bf16[4,16,128]{2,1,0:T(8,128)(2,1)S(1)}, u32[]{:S(2)}, u32[]{:S(2)}) %all-to-all-start.1) | async-done | bytes 16416 | tf_op jit(solution)/shard_map/while/body/eval_jaxpr/all_to_all | solution.py:64
  240.6 3.3 %all-to-all-start = ((bf16[4,16,128]{2,1,0:T(8,128)(2,1)}), bf16[4,16,128]{2,1,0:T(8,128)(2,1)S(1)}, u32[]{:S(2)}, u32[]{:S(2)}) async-start(bf16[4,16,128]{2,1,0:T(8,128)(2,1)} %fusion.27), calls=%async_computation | async-start | bytes 32768 | tf_op jit(solution)/shard_map/while/body/eval_jaxpr/all_to_all | solution.py:63
  244.1 3.6 %all-to-all-done = bf16[4,16,128]{2,1,0:T(8,128)(2,1)S(1)} async-done(((bf16[4,16,128]{2,1,0:T(8,128)(2,1)}), bf16[4,16,128]{2,1,0:T(8,128)(2,1)S(1)}, u32[]{:S(2)}, u32[]{:S(2)}) %all-to-all-start) | async-done | bytes 16416 | tf_op jit(solution)/shard_map/while/body/eval_jaxpr/all_to_all | solution.py:63
  249.4 5.4 %collective-permute-start = (bf16[16,1024]{1,0:T(8,128)(2,1)S(1)}, bf16[16,1024]{1,0:T(8,128)(2,1)S(1)}, u32[]{:S(2)}, u32[]{:S(2)}) collective-permute-start(bf16[16,1024]{1,0:T(8,128)(2,1)S(1)} %select_convert_fusion.5), channel_id=1, source_target_pairs={{0,4},{4,8},{8,12},{12,16},{16,20},{20,24},{24,28},{1,5},{5,9},{9,... | collective-permute-start | bytes 98312 | tf_op jit(solution)/shard_map/while/body/eval_jaxpr/ppermute | solution.py:10
  257.2 3.2 %all-to-all-start.1 = ((bf16[4,16,128]{2,1,0:T(8,128)(2,1)}), bf16[4,16,128]{2,1,0:T(8,128)(2,1)S(1)}, u32[]{:S(2)}, u32[]{:S(2)}) async-start(bf16[4,16,128]{2,1,0:T(8,128)(2,1)} %fusion.28), calls=%async_computation.1 | async-start | bytes 32768 | tf_op jit(solution)/shard_map/while/body/eval_jaxpr/all_to_all | solution.py:64
  261.5 2.8 %all-to-all-done.1 = bf16[4,16,128]{2,1,0:T(8,128)(2,1)S(1)} async-done(((bf16[4,16,128]{2,1,0:T(8,128)(2,1)}), bf16[4,16,128]{2,1,0:T(8,128)(2,1)S(1)}, u32[]{:S(2)}, u32[]{:S(2)}) %all-to-all-start.1) | async-done | bytes 16416 | tf_op jit(solution)/shard_map/while/body/eval_jaxpr/all_to_all | solution.py:64
  264.3 3.3 %all-to-all-start = ((bf16[4,16,128]{2,1,0:T(8,128)(2,1)}), bf16[4,16,128]{2,1,0:T(8,128)(2,1)S(1)}, u32[]{:S(2)}, u32[]{:S(2)}) async-start(bf16[4,16,128]{2,1,0:T(8,128)(2,1)} %fusion.27), calls=%async_computation | async-start | bytes 32768 | tf_op jit(solution)/shard_map/while/body/eval_jaxpr/all_to_all | solution.py:63
  267.8 3.6 %all-to-all-done = bf16[4,16,128]{2,1,0:T(8,128)(2,1)S(1)} async-done(((bf16[4,16,128]{2,1,0:T(8,128)(2,1)}), bf16[4,16,128]{2,1,0:T(8,128)(2,1)S(1)}, u32[]{:S(2)}, u32[]{:S(2)}) %all-to-all-start) | async-done | bytes 16416 | tf_op jit(solution)/shard_map/while/body/eval_jaxpr/all_to_all | solution.py:63
  (123 shorter events, 32.3 us)
Async XLA Ops:
  0.0 82.0 %copy-start = (bf16[1,4,128,1024]{3,2,1,0:T(8,128)(2,1)S(1)}, bf16[1,4,128,1024]{3,2,1,0:T(8,128)(2,1)}, u32[]{:S(2)}) copy-start(bf16[1,4,128,1024]{3,2,1,0:T(8,128)(2,1)} %param.13) | copy-start | bytes 3145732
  82.0 12.7 %copy-start.2 = (bf16[4,128,1024]{2,1,0:T(8,128)(2,1)S(1)}, bf16[4,128,1024]{2,1,0:T(8,128)(2,1)}, u32[]{:S(2)}) copy-start(bf16[4,128,1024]{2,1,0:T(8,128)(2,1)} %get-tuple-element.464) | copy-start | bytes 3145732 | tf_op jit(solution)/shard_map/while
  82.1 7.0 %collective-permute-start.1 = (bf16[16,1024]{1,0:T(8,128)(2,1)S(1)}, bf16[16,1024]{1,0:T(8,128)(2,1)S(1)}, u32[]{:S(2)}, u32[]{:S(2)}) collective-permute-start(bf16[16,1024]{1,0:T(8,128)(2,1)S(1)} %select_convert_fusion.6), channel_id=1, source_target_pairs={{4,0},{8,4},{12,8},{16,12},{20,16},{24,20},{28,24},{5,1},{9,5},{13... | collective-permute-start | bytes 98312 | tf_op jit(solution)/shard_map/while/body/eval_jaxpr/ppermute | solution.py:10
  83.5 11.2 %collective-permute-start = (bf16[16,1024]{1,0:T(8,128)(2,1)S(1)}, bf16[16,1024]{1,0:T(8,128)(2,1)S(1)}, u32[]{:S(2)}, u32[]{:S(2)}) collective-permute-start(bf16[16,1024]{1,0:T(8,128)(2,1)S(1)} %select_convert_fusion.5), channel_id=1, source_target_pairs={{0,4},{4,8},{8,12},{12,16},{16,20},{20,24},{24,28},{1,5},{5,9},{9,... | collective-permute-start | bytes 98312 | tf_op jit(solution)/shard_map/while/body/eval_jaxpr/ppermute | solution.py:10
  89.1 12.7 %copy-start.1 = (bf16[1,4,128,1024]{3,2,1,0:T(8,128)(2,1)S(1)}, bf16[1,4,128,1024]{3,2,1,0:T(8,128)(2,1)}, u32[]{:S(2)}) copy-start(bf16[1,4,128,1024]{3,2,1,0:T(8,128)(2,1)} %get-tuple-element.469) | copy-start | bytes 3145732 | tf_op jit(solution)/shard_map/while
  91.4 7.2 %all-to-all-start.1 = ((bf16[4,16,128]{2,1,0:T(8,128)(2,1)}), bf16[4,16,128]{2,1,0:T(8,128)(2,1)S(1)}, u32[]{:S(2)}, u32[]{:S(2)}) async-start(bf16[4,16,128]{2,1,0:T(8,128)(2,1)} %fusion.28), calls=%async_computation.1 | async-start | bytes 32768 | tf_op jit(solution)/shard_map/while/body/eval_jaxpr/all_to_all | solution.py:64
  98.6 7.1 %all-to-all-start = ((bf16[4,16,128]{2,1,0:T(8,128)(2,1)}), bf16[4,16,128]{2,1,0:T(8,128)(2,1)S(1)}, u32[]{:S(2)}, u32[]{:S(2)}) async-start(bf16[4,16,128]{2,1,0:T(8,128)(2,1)} %fusion.27), calls=%async_computation | async-start | bytes 32768 | tf_op jit(solution)/shard_map/while/body/eval_jaxpr/all_to_all | solution.py:63
  105.9 6.8 %collective-permute-start.1 = (bf16[16,1024]{1,0:T(8,128)(2,1)S(1)}, bf16[16,1024]{1,0:T(8,128)(2,1)S(1)}, u32[]{:S(2)}, u32[]{:S(2)}) collective-permute-start(bf16[16,1024]{1,0:T(8,128)(2,1)S(1)} %select_convert_fusion.6), channel_id=1, source_target_pairs={{4,0},{8,4},{12,8},{16,12},{20,16},{24,20},{28,24},{5,1},{9,5},{13... | collective-permute-start | bytes 98312 | tf_op jit(solution)/shard_map/while/body/eval_jaxpr/ppermute | solution.py:10
  107.4 11.0 %collective-permute-start = (bf16[16,1024]{1,0:T(8,128)(2,1)S(1)}, bf16[16,1024]{1,0:T(8,128)(2,1)S(1)}, u32[]{:S(2)}, u32[]{:S(2)}) collective-permute-start(bf16[16,1024]{1,0:T(8,128)(2,1)S(1)} %select_convert_fusion.5), channel_id=1, source_target_pairs={{0,4},{4,8},{8,12},{12,16},{16,20},{20,24},{24,28},{1,5},{5,9},{9,... | collective-permute-start | bytes 98312 | tf_op jit(solution)/shard_map/while/body/eval_jaxpr/ppermute | solution.py:10
  112.8 12.7 %copy-start.1 = (bf16[1,4,128,1024]{3,2,1,0:T(8,128)(2,1)S(1)}, bf16[1,4,128,1024]{3,2,1,0:T(8,128)(2,1)}, u32[]{:S(2)}) copy-start(bf16[1,4,128,1024]{3,2,1,0:T(8,128)(2,1)} %get-tuple-element.469) | copy-start | bytes 3145732 | tf_op jit(solution)/shard_map/while
  115.1 7.1 %all-to-all-start.1 = ((bf16[4,16,128]{2,1,0:T(8,128)(2,1)}), bf16[4,16,128]{2,1,0:T(8,128)(2,1)S(1)}, u32[]{:S(2)}, u32[]{:S(2)}) async-start(bf16[4,16,128]{2,1,0:T(8,128)(2,1)} %fusion.28), calls=%async_computation.1 | async-start | bytes 32768 | tf_op jit(solution)/shard_map/while/body/eval_jaxpr/all_to_all | solution.py:64
  122.2 7.1 %all-to-all-start = ((bf16[4,16,128]{2,1,0:T(8,128)(2,1)}), bf16[4,16,128]{2,1,0:T(8,128)(2,1)S(1)}, u32[]{:S(2)}, u32[]{:S(2)}) async-start(bf16[4,16,128]{2,1,0:T(8,128)(2,1)} %fusion.27), calls=%async_computation | async-start | bytes 32768 | tf_op jit(solution)/shard_map/while/body/eval_jaxpr/all_to_all | solution.py:63
  129.5 12.5 %copy-start.2 = (bf16[4,128,1024]{2,1,0:T(8,128)(2,1)S(1)}, bf16[4,128,1024]{2,1,0:T(8,128)(2,1)}, u32[]{:S(2)}) copy-start(bf16[4,128,1024]{2,1,0:T(8,128)(2,1)} %get-tuple-element.464) | copy-start | bytes 3145732 | tf_op jit(solution)/shard_map/while
  129.5 6.9 %collective-permute-start.1 = (bf16[16,1024]{1,0:T(8,128)(2,1)S(1)}, bf16[16,1024]{1,0:T(8,128)(2,1)S(1)}, u32[]{:S(2)}, u32[]{:S(2)}) collective-permute-start(bf16[16,1024]{1,0:T(8,128)(2,1)S(1)} %select_convert_fusion.6), channel_id=1, source_target_pairs={{4,0},{8,4},{12,8},{16,12},{20,16},{24,20},{28,24},{5,1},{9,5},{13... | collective-permute-start | bytes 98312 | tf_op jit(solution)/shard_map/while/body/eval_jaxpr/ppermute | solution.py:10
  131.0 11.1 %collective-permute-start = (bf16[16,1024]{1,0:T(8,128)(2,1)S(1)}, bf16[16,1024]{1,0:T(8,128)(2,1)S(1)}, u32[]{:S(2)}, u32[]{:S(2)}) collective-permute-start(bf16[16,1024]{1,0:T(8,128)(2,1)S(1)} %select_convert_fusion.5), channel_id=1, source_target_pairs={{0,4},{4,8},{8,12},{12,16},{16,20},{20,24},{24,28},{1,5},{5,9},{9,... | collective-permute-start | bytes 98312 | tf_op jit(solution)/shard_map/while/body/eval_jaxpr/ppermute | solution.py:10
  136.5 12.7 %copy-start.1 = (bf16[1,4,128,1024]{3,2,1,0:T(8,128)(2,1)S(1)}, bf16[1,4,128,1024]{3,2,1,0:T(8,128)(2,1)}, u32[]{:S(2)}) copy-start(bf16[1,4,128,1024]{3,2,1,0:T(8,128)(2,1)} %get-tuple-element.469) | copy-start | bytes 3145732 | tf_op jit(solution)/shard_map/while
  138.8 7.1 %all-to-all-start.1 = ((bf16[4,16,128]{2,1,0:T(8,128)(2,1)}), bf16[4,16,128]{2,1,0:T(8,128)(2,1)S(1)}, u32[]{:S(2)}, u32[]{:S(2)}) async-start(bf16[4,16,128]{2,1,0:T(8,128)(2,1)} %fusion.28), calls=%async_computation.1 | async-start | bytes 32768 | tf_op jit(solution)/shard_map/while/body/eval_jaxpr/all_to_all | solution.py:64
  145.8 7.1 %all-to-all-start = ((bf16[4,16,128]{2,1,0:T(8,128)(2,1)}), bf16[4,16,128]{2,1,0:T(8,128)(2,1)S(1)}, u32[]{:S(2)}, u32[]{:S(2)}) async-start(bf16[4,16,128]{2,1,0:T(8,128)(2,1)} %fusion.27), calls=%async_computation | async-start | bytes 32768 | tf_op jit(solution)/shard_map/while/body/eval_jaxpr/all_to_all | solution.py:63
  153.2 12.5 %copy-start.2 = (bf16[4,128,1024]{2,1,0:T(8,128)(2,1)S(1)}, bf16[4,128,1024]{2,1,0:T(8,128)(2,1)}, u32[]{:S(2)}) copy-start(bf16[4,128,1024]{2,1,0:T(8,128)(2,1)} %get-tuple-element.464) | copy-start | bytes 3145732 | tf_op jit(solution)/shard_map/while
  153.2 6.9 %collective-permute-start.1 = (bf16[16,1024]{1,0:T(8,128)(2,1)S(1)}, bf16[16,1024]{1,0:T(8,128)(2,1)S(1)}, u32[]{:S(2)}, u32[]{:S(2)}) collective-permute-start(bf16[16,1024]{1,0:T(8,128)(2,1)S(1)} %select_convert_fusion.6), channel_id=1, source_target_pairs={{4,0},{8,4},{12,8},{16,12},{20,16},{24,20},{28,24},{5,1},{9,5},{13... | collective-permute-start | bytes 98312 | tf_op jit(solution)/shard_map/while/body/eval_jaxpr/ppermute | solution.py:10
  154.6 11.1 %collective-permute-start = (bf16[16,1024]{1,0:T(8,128)(2,1)S(1)}, bf16[16,1024]{1,0:T(8,128)(2,1)S(1)}, u32[]{:S(2)}, u32[]{:S(2)}) collective-permute-start(bf16[16,1024]{1,0:T(8,128)(2,1)S(1)} %select_convert_fusion.5), channel_id=1, source_target_pairs={{0,4},{4,8},{8,12},{12,16},{16,20},{20,24},{24,28},{1,5},{5,9},{9,... | collective-permute-start | bytes 98312 | tf_op jit(solution)/shard_map/while/body/eval_jaxpr/ppermute | solution.py:10
  160.1 12.7 %copy-start.1 = (bf16[1,4,128,1024]{3,2,1,0:T(8,128)(2,1)S(1)}, bf16[1,4,128,1024]{3,2,1,0:T(8,128)(2,1)}, u32[]{:S(2)}) copy-start(bf16[1,4,128,1024]{3,2,1,0:T(8,128)(2,1)} %get-tuple-element.469) | copy-start | bytes 3145732 | tf_op jit(solution)/shard_map/while
  162.5 7.1 %all-to-all-start.1 = ((bf16[4,16,128]{2,1,0:T(8,128)(2,1)}), bf16[4,16,128]{2,1,0:T(8,128)(2,1)S(1)}, u32[]{:S(2)}, u32[]{:S(2)}) async-start(bf16[4,16,128]{2,1,0:T(8,128)(2,1)} %fusion.28), calls=%async_computation.1 | async-start | bytes 32768 | tf_op jit(solution)/shard_map/while/body/eval_jaxpr/all_to_all | solution.py:64
  169.5 7.1 %all-to-all-start = ((bf16[4,16,128]{2,1,0:T(8,128)(2,1)}), bf16[4,16,128]{2,1,0:T(8,128)(2,1)S(1)}, u32[]{:S(2)}, u32[]{:S(2)}) async-start(bf16[4,16,128]{2,1,0:T(8,128)(2,1)} %fusion.27), calls=%async_computation | async-start | bytes 32768 | tf_op jit(solution)/shard_map/while/body/eval_jaxpr/all_to_all | solution.py:63
  176.9 12.5 %copy-start.2 = (bf16[4,128,1024]{2,1,0:T(8,128)(2,1)S(1)}, bf16[4,128,1024]{2,1,0:T(8,128)(2,1)}, u32[]{:S(2)}) copy-start(bf16[4,128,1024]{2,1,0:T(8,128)(2,1)} %get-tuple-element.464) | copy-start | bytes 3145732 | tf_op jit(solution)/shard_map/while
  176.9 6.9 %collective-permute-start.1 = (bf16[16,1024]{1,0:T(8,128)(2,1)S(1)}, bf16[16,1024]{1,0:T(8,128)(2,1)S(1)}, u32[]{:S(2)}, u32[]{:S(2)}) collective-permute-start(bf16[16,1024]{1,0:T(8,128)(2,1)S(1)} %select_convert_fusion.6), channel_id=1, source_target_pairs={{4,0},{8,4},{12,8},{16,12},{20,16},{24,20},{28,24},{5,1},{9,5},{13... | collective-permute-start | bytes 98312 | tf_op jit(solution)/shard_map/while/body/eval_jaxpr/ppermute | solution.py:10
  178.3 11.1 %collective-permute-start = (bf16[16,1024]{1,0:T(8,128)(2,1)S(1)}, bf16[16,1024]{1,0:T(8,128)(2,1)S(1)}, u32[]{:S(2)}, u32[]{:S(2)}) collective-permute-start(bf16[16,1024]{1,0:T(8,128)(2,1)S(1)} %select_convert_fusion.5), channel_id=1, source_target_pairs={{0,4},{4,8},{8,12},{12,16},{16,20},{20,24},{24,28},{1,5},{5,9},{9,... | collective-permute-start | bytes 98312 | tf_op jit(solution)/shard_map/while/body/eval_jaxpr/ppermute | solution.py:10
  183.8 12.7 %copy-start.1 = (bf16[1,4,128,1024]{3,2,1,0:T(8,128)(2,1)S(1)}, bf16[1,4,128,1024]{3,2,1,0:T(8,128)(2,1)}, u32[]{:S(2)}) copy-start(bf16[1,4,128,1024]{3,2,1,0:T(8,128)(2,1)} %get-tuple-element.469) | copy-start | bytes 3145732 | tf_op jit(solution)/shard_map/while
  186.2 7.1 %all-to-all-start.1 = ((bf16[4,16,128]{2,1,0:T(8,128)(2,1)}), bf16[4,16,128]{2,1,0:T(8,128)(2,1)S(1)}, u32[]{:S(2)}, u32[]{:S(2)}) async-start(bf16[4,16,128]{2,1,0:T(8,128)(2,1)} %fusion.28), calls=%async_computation.1 | async-start | bytes 32768 | tf_op jit(solution)/shard_map/while/body/eval_jaxpr/all_to_all | solution.py:64
  193.2 7.1 %all-to-all-start = ((bf16[4,16,128]{2,1,0:T(8,128)(2,1)}), bf16[4,16,128]{2,1,0:T(8,128)(2,1)S(1)}, u32[]{:S(2)}, u32[]{:S(2)}) async-start(bf16[4,16,128]{2,1,0:T(8,128)(2,1)} %fusion.27), calls=%async_computation | async-start | bytes 32768 | tf_op jit(solution)/shard_map/while/body/eval_jaxpr/all_to_all | solution.py:63
  200.6 12.5 %copy-start.2 = (bf16[4,128,1024]{2,1,0:T(8,128)(2,1)S(1)}, bf16[4,128,1024]{2,1,0:T(8,128)(2,1)}, u32[]{:S(2)}) copy-start(bf16[4,128,1024]{2,1,0:T(8,128)(2,1)} %get-tuple-element.464) | copy-start | bytes 3145732 | tf_op jit(solution)/shard_map/while
  200.6 6.9 %collective-permute-start.1 = (bf16[16,1024]{1,0:T(8,128)(2,1)S(1)}, bf16[16,1024]{1,0:T(8,128)(2,1)S(1)}, u32[]{:S(2)}, u32[]{:S(2)}) collective-permute-start(bf16[16,1024]{1,0:T(8,128)(2,1)S(1)} %select_convert_fusion.6), channel_id=1, source_target_pairs={{4,0},{8,4},{12,8},{16,12},{20,16},{24,20},{28,24},{5,1},{9,5},{13... | collective-permute-start | bytes 98312 | tf_op jit(solution)/shard_map/while/body/eval_jaxpr/ppermute | solution.py:10
  202.0 11.1 %collective-permute-start = (bf16[16,1024]{1,0:T(8,128)(2,1)S(1)}, bf16[16,1024]{1,0:T(8,128)(2,1)S(1)}, u32[]{:S(2)}, u32[]{:S(2)}) collective-permute-start(bf16[16,1024]{1,0:T(8,128)(2,1)S(1)} %select_convert_fusion.5), channel_id=1, source_target_pairs={{0,4},{4,8},{8,12},{12,16},{16,20},{20,24},{24,28},{1,5},{5,9},{9,... | collective-permute-start | bytes 98312 | tf_op jit(solution)/shard_map/while/body/eval_jaxpr/ppermute | solution.py:10
  207.5 12.7 %copy-start.1 = (bf16[1,4,128,1024]{3,2,1,0:T(8,128)(2,1)S(1)}, bf16[1,4,128,1024]{3,2,1,0:T(8,128)(2,1)}, u32[]{:S(2)}) copy-start(bf16[1,4,128,1024]{3,2,1,0:T(8,128)(2,1)} %get-tuple-element.469) | copy-start | bytes 3145732 | tf_op jit(solution)/shard_map/while
  209.8 7.1 %all-to-all-start.1 = ((bf16[4,16,128]{2,1,0:T(8,128)(2,1)}), bf16[4,16,128]{2,1,0:T(8,128)(2,1)S(1)}, u32[]{:S(2)}, u32[]{:S(2)}) async-start(bf16[4,16,128]{2,1,0:T(8,128)(2,1)} %fusion.28), calls=%async_computation.1 | async-start | bytes 32768 | tf_op jit(solution)/shard_map/while/body/eval_jaxpr/all_to_all | solution.py:64
  216.9 7.1 %all-to-all-start = ((bf16[4,16,128]{2,1,0:T(8,128)(2,1)}), bf16[4,16,128]{2,1,0:T(8,128)(2,1)S(1)}, u32[]{:S(2)}, u32[]{:S(2)}) async-start(bf16[4,16,128]{2,1,0:T(8,128)(2,1)} %fusion.27), calls=%async_computation | async-start | bytes 32768 | tf_op jit(solution)/shard_map/while/body/eval_jaxpr/all_to_all | solution.py:63
  224.3 12.5 %copy-start.2 = (bf16[4,128,1024]{2,1,0:T(8,128)(2,1)S(1)}, bf16[4,128,1024]{2,1,0:T(8,128)(2,1)}, u32[]{:S(2)}) copy-start(bf16[4,128,1024]{2,1,0:T(8,128)(2,1)} %get-tuple-element.464) | copy-start | bytes 3145732 | tf_op jit(solution)/shard_map/while
  224.3 6.9 %collective-permute-start.1 = (bf16[16,1024]{1,0:T(8,128)(2,1)S(1)}, bf16[16,1024]{1,0:T(8,128)(2,1)S(1)}, u32[]{:S(2)}, u32[]{:S(2)}) collective-permute-start(bf16[16,1024]{1,0:T(8,128)(2,1)S(1)} %select_convert_fusion.6), channel_id=1, source_target_pairs={{4,0},{8,4},{12,8},{16,12},{20,16},{24,20},{28,24},{5,1},{9,5},{13... | collective-permute-start | bytes 98312 | tf_op jit(solution)/shard_map/while/body/eval_jaxpr/ppermute | solution.py:10
  225.7 11.1 %collective-permute-start = (bf16[16,1024]{1,0:T(8,128)(2,1)S(1)}, bf16[16,1024]{1,0:T(8,128)(2,1)S(1)}, u32[]{:S(2)}, u32[]{:S(2)}) collective-permute-start(bf16[16,1024]{1,0:T(8,128)(2,1)S(1)} %select_convert_fusion.5), channel_id=1, source_target_pairs={{0,4},{4,8},{8,12},{12,16},{16,20},{20,24},{24,28},{1,5},{5,9},{9,... | collective-permute-start | bytes 98312 | tf_op jit(solution)/shard_map/while/body/eval_jaxpr/ppermute | solution.py:10
  231.2 12.7 %copy-start.1 = (bf16[1,4,128,1024]{3,2,1,0:T(8,128)(2,1)S(1)}, bf16[1,4,128,1024]{3,2,1,0:T(8,128)(2,1)}, u32[]{:S(2)}) copy-start(bf16[1,4,128,1024]{3,2,1,0:T(8,128)(2,1)} %get-tuple-element.469) | copy-start | bytes 3145732 | tf_op jit(solution)/shard_map/while
  233.5 7.1 %all-to-all-start.1 = ((bf16[4,16,128]{2,1,0:T(8,128)(2,1)}), bf16[4,16,128]{2,1,0:T(8,128)(2,1)S(1)}, u32[]{:S(2)}, u32[]{:S(2)}) async-start(bf16[4,16,128]{2,1,0:T(8,128)(2,1)} %fusion.28), calls=%async_computation.1 | async-start | bytes 32768 | tf_op jit(solution)/shard_map/while/body/eval_jaxpr/all_to_all | solution.py:64
  240.6 7.1 %all-to-all-start = ((bf16[4,16,128]{2,1,0:T(8,128)(2,1)}), bf16[4,16,128]{2,1,0:T(8,128)(2,1)S(1)}, u32[]{:S(2)}, u32[]{:S(2)}) async-start(bf16[4,16,128]{2,1,0:T(8,128)(2,1)} %fusion.27), calls=%async_computation | async-start | bytes 32768 | tf_op jit(solution)/shard_map/while/body/eval_jaxpr/all_to_all | solution.py:63
  247.9 12.5 %copy-start.2 = (bf16[4,128,1024]{2,1,0:T(8,128)(2,1)S(1)}, bf16[4,128,1024]{2,1,0:T(8,128)(2,1)}, u32[]{:S(2)}) copy-start(bf16[4,128,1024]{2,1,0:T(8,128)(2,1)} %get-tuple-element.464) | copy-start | bytes 3145732 | tf_op jit(solution)/shard_map/while
  248.0 6.9 %collective-permute-start.1 = (bf16[16,1024]{1,0:T(8,128)(2,1)S(1)}, bf16[16,1024]{1,0:T(8,128)(2,1)S(1)}, u32[]{:S(2)}, u32[]{:S(2)}) collective-permute-start(bf16[16,1024]{1,0:T(8,128)(2,1)S(1)} %select_convert_fusion.6), channel_id=1, source_target_pairs={{4,0},{8,4},{12,8},{16,12},{20,16},{24,20},{28,24},{5,1},{9,5},{13... | collective-permute-start | bytes 98312 | tf_op jit(solution)/shard_map/while/body/eval_jaxpr/ppermute | solution.py:10
  249.4 11.1 %collective-permute-start = (bf16[16,1024]{1,0:T(8,128)(2,1)S(1)}, bf16[16,1024]{1,0:T(8,128)(2,1)S(1)}, u32[]{:S(2)}, u32[]{:S(2)}) collective-permute-start(bf16[16,1024]{1,0:T(8,128)(2,1)S(1)} %select_convert_fusion.5), channel_id=1, source_target_pairs={{0,4},{4,8},{8,12},{12,16},{16,20},{20,24},{24,28},{1,5},{5,9},{9,... | collective-permute-start | bytes 98312 | tf_op jit(solution)/shard_map/while/body/eval_jaxpr/ppermute | solution.py:10
  254.9 12.7 %copy-start.1 = (bf16[1,4,128,1024]{3,2,1,0:T(8,128)(2,1)S(1)}, bf16[1,4,128,1024]{3,2,1,0:T(8,128)(2,1)}, u32[]{:S(2)}) copy-start(bf16[1,4,128,1024]{3,2,1,0:T(8,128)(2,1)} %get-tuple-element.469) | copy-start | bytes 3145732 | tf_op jit(solution)/shard_map/while
  257.2 7.1 %all-to-all-start.1 = ((bf16[4,16,128]{2,1,0:T(8,128)(2,1)}), bf16[4,16,128]{2,1,0:T(8,128)(2,1)S(1)}, u32[]{:S(2)}, u32[]{:S(2)}) async-start(bf16[4,16,128]{2,1,0:T(8,128)(2,1)} %fusion.28), calls=%async_computation.1 | async-start | bytes 32768 | tf_op jit(solution)/shard_map/while/body/eval_jaxpr/all_to_all | solution.py:64
  264.3 7.1 %all-to-all-start = ((bf16[4,16,128]{2,1,0:T(8,128)(2,1)}), bf16[4,16,128]{2,1,0:T(8,128)(2,1)S(1)}, u32[]{:S(2)}, u32[]{:S(2)}) async-start(bf16[4,16,128]{2,1,0:T(8,128)(2,1)} %fusion.27), calls=%async_computation | async-start | bytes 32768 | tf_op jit(solution)/shard_map/while/body/eval_jaxpr/all_to_all | solution.py:63
  (3 other events, 13.8 us)
where the time goes:
time: 274 us; the launch traced here: 272 us
  starting transfers between devices  107 us (39%)
  other arithmetic  80.7 us (29%)
  waiting for transfers between devices  51 us (19%)
  matrix products  30.9 us (11%)
    another operation x3, other arithmetic, front_solve(): jax.scipy.linalg.solve_triangular(front_blocks, stacked, lower=True)  79.8 us
    ppermute x16, starting transfers between devices, shifted(): return lax.ppermute(value, axis, pairs)  54.9 us
    all_to_all x8, waiting for transfers between devices, advance(): lax.all_to_all(down_coeffs, 'plane', split_axis=0, concat_axis=0, tiled=T...  28.5 us
    dot_general x16, matrix products, compress(): jnp.einsum('ikt,st->isk', factor_in, trace.astype(jnp.bfloat16), preferre...  26.4 us
    all_to_all x8, starting transfers between devices, advance(): lax.all_to_all(down_coeffs, 'plane', split_axis=0, concat_axis=0, tiled=T...  26 us
    all_to_all x8, starting transfers between devices, advance(): lax.all_to_all(up_coeffs, 'plane', split_axis=0, concat_axis=0, tiled=True)  26 us
    all_to_all x8, waiting for transfers between devices, advance(): lax.all_to_all(up_coeffs, 'plane', split_axis=0, concat_axis=0, tiled=True)  22.5 us
  transfers between devices with their start and end apart: 32, of which 16 were waited for; matrix products, arithmetic and copies ran while one was open for 10% of the time, Pallas kernels for 0%

commit v1 on v0

v1 whole, which is shorter than its diff:
```python
import functools

import jax
import jax.numpy as jnp
from jax import lax
from jax.experimental import pallas as pl
from jax.experimental.pallas import tpu as pltpu
from jax.sharding import PartitionSpec as P


def solve_kernel(source_ref, front_ref, out_ref):
    blocks, size, _ = front_ref.shape
    row = lax.broadcasted_iota(jnp.int32, (size, size), 0)
    col = lax.broadcasted_iota(jnp.int32, (size, size), 1)
    state, lower = [], []
    for b in range(blocks):
        turned = front_ref[b].T
        diagonal = jnp.sum(jnp.where(row == col, turned, 0.0), axis=0, keepdims=True)
        scale = 1.0 / diagonal
        lower.append(jnp.where(row < col, turned * scale, 0.0))
        state.append(source_ref[:, b * size : (b + 1) * size] * scale)
    for t in range(size - 1):
        for b in range(blocks):
            state[b] = state[b] - state[b][:, t : t + 1] * lower[b][t : t + 1, :]
    for b in range(blocks):
        out_ref[:, b * size : (b + 1) * size] = state[b]


def front_solve(source, front_blocks):
    return pl.pallas_call(
        solve_kernel,
        out_shape=jax.ShapeDtypeStruct(source.shape, jnp.float32),
        in_specs=[pl.BlockSpec(memory_space=pltpu.VMEM)] * 2,
        out_specs=pl.BlockSpec(memory_space=pltpu.VMEM),
        compiler_params=pltpu.CompilerParams(vmem_limit_bytes=16 * 2**20),
        name="front_solve",
    )(source, front_blocks)


def compress(trace, factor_in):
    return jnp.einsum(
        "ikt,st->isk", factor_in, trace, preferred_element_type=jnp.float32
    ).astype(jnp.bfloat16)


def expand(coeffs, factor_out, keep_mask):
    return jnp.einsum(
        "jsk,jkt->st",
        coeffs * keep_mask[:, None, :],
        factor_out,
        preferred_element_type=jnp.float32,
    )


def shards(layers, planes, sources, fronts, down_left, down_right, up_left, up_right, ranks, pattern):
    solved = front_solve(sources[0], fronts[0])
    layer_at = lax.axis_index("layer")
    rank_top = down_left.shape[2]
    ladder = jnp.arange(rank_top, dtype=jnp.int32)
    keep_mask = (
        pattern[0, :, 0, :, None]
        * (ladder[None, None, :] < ranks[0, :, 0, :, None]).astype(jnp.int32)
    ).astype(jnp.bfloat16)

    half = layers // 2
    down_first = layer_at < half
    lefts = (
        jnp.where(down_first, down_left[0], up_left[0]),
        jnp.where(down_first, up_left[0], down_left[0]),
    )
    rights = (
        jnp.where(down_first, down_right[0], up_right[0]),
        jnp.where(down_first, up_right[0], down_right[0]),
    )
    keeps = (
        jnp.where(down_first, keep_mask[0], keep_mask[1]),
        jnp.where(down_first, keep_mask[1], keep_mask[0]),
    )

    trace = solved
    results = [solved, solved]
    for turn in range(layers - 1):
        which = 0 if turn < half - 1 else 1
        pairs = []
        for plane in range(planes):
            pairs.append((turn * planes + plane, (turn + 1) * planes + plane))
            pairs.append(((layers - 1 - turn) * planes + plane, (layers - 2 - turn) * planes + plane))
        arrived = lax.ppermute(trace.astype(jnp.bfloat16), ("layer", "plane"), pairs)
        coeffs = compress(arrived, lefts[which])
        coeffs = lax.all_to_all(coeffs, "plane", split_axis=0, concat_axis=0, tiled=True)
        trace = solved + expand(coeffs, rights[which], keeps[which])
        active = (layer_at == turn + 1) | (layer_at == layers - 2 - turn)
        results[which] = jnp.where(active, trace, results[which])
    field = results[0] + results[1] - solved
    return field[None]


def solution(mesh):
    layers, planes = mesh.shape["layer"], mesh.shape["plane"]
    in_specs = (
        P("layer", None, "plane"),
        P("layer", "plane", None, None),
        P("layer", None, None, "plane"),
        P("layer", None, None, "plane"),
        P("layer", None, None, "plane"),
        P("layer", None, None, "plane"),
        P("layer", None, "plane", None),
        P("layer", None, "plane", None),
    )
    out_specs = P("layer", None, "plane")
    return jax.shard_map(
        functools.partial(shards, layers, planes),
        mesh=mesh,
        in_specs=in_specs,
        out_specs=out_specs,
        check_vma=False,
    )
```

time: 274 us -> 99.8 us (0.36)
  starting transfers between devices: 107 us -> 16.1 us
  other arithmetic: 80.7 us -> 2.05 us
  blocking collectives: 0 us -> 31.1 us
  matrix products: 30.9 us -> 6.26 us
  waiting for transfers between devices: 51 us -> 31.2 us
  Pallas kernels: 0 us -> 9.04 us
    another operation x3 -> x0, other arithmetic: 79.8 us -> none  [front_solve(): jax.scipy.linalg.solve_triangular(front_blocks, stacked, lower=True)]
    all_to_all x16 -> x2, starting transfers between devices: 52.1 us -> 6.51 us  [shards(): lax.all_to_all(coeffs, 'plane', split_axis=0, concat_axis=0, tiled=True)]
    ppermute x16 -> x7, starting transfers between devices: 54.9 us -> 9.57 us  [shards(): lax.ppermute(trace.astype(jnp.bfloat16), ('layer', 'plane'), pairs)]
    all_to_all x16 -> x2, waiting for transfers between devices: 51 us -> 7.61 us  [shards(): lax.all_to_all(coeffs, 'plane', split_axis=0, concat_axis=0, tiled=True)]
    all_to_all x0 -> x5, blocking collectives: none -> 31.1 us  [shards(): lax.all_to_all(coeffs, 'plane', split_axis=0, concat_axis=0, tiled=True)]
    ppermute x16 -> x7, waiting for transfers between devices: 0.04 us -> 23.6 us  [shards(): lax.ppermute(trace.astype(jnp.bfloat16), ('layer', 'plane'), pairs)]
    dot_general x16 -> x7, matrix products: 26.4 us -> 3.86 us  [compress(): jnp.einsum('ikt,st->isk', factor_in, trace, preferred_element_type=jnp.fl...]
    pallas_call x0 -> x1, Pallas kernels: none -> 9.04 us  [front_solve(): pl.pallas_call(solve_kernel, out_shape=jax.ShapeDtypeStruct(source.shape,...]
  transfers between devices with their start and end apart: 32 -> 9, of which waited for: 16 -> 3; matrix products, arithmetic and copies ran while one was open for 10% -> 2% of each run, Pallas kernels for 0% -> 0%
where the time goes in v1:
time: 99.8 us; the launch traced here: 99.1 us
  waiting for transfers between devices  31.2 us (31%)
  blocking collectives  31.1 us (31%)
  starting transfers between devices  16.1 us (16%)
  Pallas kernels  9.04 us (9%)
  matrix products  6.26 us (6%)
  local copies, waits for them, and re-layouts  3.29 us (3%)
  other arithmetic  2.05 us (2%)
    all_to_all x5, blocking collectives, shards(): lax.all_to_all(coeffs, 'plane', split_axis=0, concat_axis=0, tiled=True)  31.1 us
    ppermute x7, waiting for transfers between devices, shards(): lax.ppermute(trace.astype(jnp.bfloat16), ('layer', 'plane'), pairs)  23.6 us
    ppermute x7, starting transfers between devices, shards(): lax.ppermute(trace.astype(jnp.bfloat16), ('layer', 'plane'), pairs)  9.57 us
    pallas_call x1, Pallas kernels, front_solve(): pl.pallas_call(solve_kernel, out_shape=jax.ShapeDtypeStruct(source.shape,...  9.04 us
    all_to_all x2, waiting for transfers between devices, shards(): lax.all_to_all(coeffs, 'plane', split_axis=0, concat_axis=0, tiled=True)  7.61 us
    all_to_all x2, starting transfers between devices, shards(): lax.all_to_all(coeffs, 'plane', split_axis=0, concat_axis=0, tiled=True)  6.51 us
    dot_general x7, matrix products, compress(): jnp.einsum('ikt,st->isk', factor_in, trace, preferred_element_type=jnp.fl...  3.86 us
    unnamed x16, local copies, waits for them, and re-layouts  3.29 us
  transfers between devices with their start and end apart: 9, of which 3 were waited for; matrix products, arithmetic and copies ran while one was open for 2% of the time, Pallas kernels for 0%

profile of v1, /device:TPU:0, one launch (start us, length us, event | category | flops | bytes accessed | tf_op | source)
XLA Modules:
  0.0 99.1 jit_solution(3100242022134101931)
XLA Ops:
  0.0 1.0 %copy-done = f32[1,8,128,128]{3,2,1,0:T(8,128)S(1)} copy-done((f32[1,8,128,128]{3,2,1,0:T(8,128)S(1)}, f32[1,8,128,128]{3,2,1,0:T(8,128)}, u32[]{:S(2)}) %copy-start) | copy-done | bytes 524312
  1.0 0.8 copy-done.1
  1.9 9.0 %front_solve.1 = f32[16,1024]{1,0:T(8,128)S(1)} custom-call(f32[16,1024]{1,0:T(8,128)S(1)} %bitcast.126, f32[8,128,128]{2,1,0:T(8,128)S(1)} %bitcast.125), custom_call_target="tpu_custom_call" | custom-call | tf_op jit(solution)/shard_map/front_solve/pallas_call | solution.py:30
  10.9 4.9 %collective-permute-start = (bf16[16,1024]{1,0:T(8,128)(2,1)S(1)}, bf16[16,1024]{1,0:T(8,128)(2,1)S(1)}, u32[]{:S(2)}, u32[]{:S(2)}) collective-permute-start(bf16[16,1024]{1,0:T(8,128)(2,1)S(1)} %convert_element_type.67), channel_id=1, source_target_pairs={{0,4},{28,24},{1,5},{29,25},{2,6},{30,26},{3,7},{31,27}} | collective-permute-start | bytes 98312 | tf_op jit(solution)/shard_map/ppermute | solution.py:88
  15.8 0.0 copy-start.4
  15.8 0.0 copy-start.5
  15.8 1.8 %broadcast_select_fusion.2 = (bf16[1,4,128,1024]{3,2,1,0:T(8,128)(2,1)S(1)}, bf16[1,4,128,1024]{3,2,1,0:T(8,128)(2,1)S(1)}) fusion(bf16[1,4,128,1024]{3,2,1,0:T(8,128)(2,1)} %param.11, bf16[1,4,128,1024]{3,2,1,0:T(8,128)(2,1)} %param.13, pred[]{:T(512)S(6)} %lt.18), kind=kLoop, calls=%fused_computation.48 | loop fusion | flops 1048576 | bytes 4194305 | tf_op jit(solution)/shard_map/jit(_where)/select_n | solution.py:72
  17.7 0.0 copy-done.4
  17.7 0.3 copy-done.5
  18.0 0.1 broadcast_select_fusion.3
  18.1 0.0 copy-start.6
  18.2 0.5 copy-done.7
  18.7 0.2 copy-done.6
  18.9 0.1 select_convert_fusion
  18.9 0.0 collective-permute-done
  18.9 0.2 copy-done.2
  19.1 1.0 %fusion.11 = bf16[4,16,128]{2,1,0:T(8,128)(2,1)} fusion(bf16[1,4,128,1024]{3,2,1,0:T(8,128)(2,1)S(1)} %get-tuple-element.5, bf16[16,1024]{1,0:T(8,128)(2,1)S(1)} %collective-permute-done), kind=kOutput, calls=%fused_computation.25 | convolution fusion | flops 16785408 | bytes 1097728 | tf_op jit(solution)/shard_map/ikt,st->isk/dot_general | solution.py:41
  20.1 3.3 %all-to-all-start = ((bf16[4,16,128]{2,1,0:T(8,128)(2,1)}), bf16[4,16,128]{2,1,0:T(8,128)(2,1)S(1)}, u32[]{:S(2)}, u32[]{:S(2)}) async-start(bf16[4,16,128]{2,1,0:T(8,128)(2,1)} %fusion.11), calls=%async_computation | async-start | bytes 32768 | tf_op jit(solution)/shard_map/all_to_all | solution.py:90
  23.4 3.8 %all-to-all-done = bf16[4,16,128]{2,1,0:T(8,128)(2,1)S(1)} async-done(((bf16[4,16,128]{2,1,0:T(8,128)(2,1)}), bf16[4,16,128]{2,1,0:T(8,128)(2,1)S(1)}, u32[]{:S(2)}, u32[]{:S(2)}) %all-to-all-start) | async-done | bytes 16416 | tf_op jit(solution)/shard_map/all_to_all | solution.py:90
  27.2 0.3 fusion.53
  27.5 0.8 collective-permute-start.1
  28.3 0.0 collective-permute-done.1
  28.3 0.2 copy-done.3
  28.5 0.4 fusion.12
  28.8 6.2 %all_to_all.35 = bf16[4,16,128]{2,1,0:T(8,128)(2,1)S(1)} all-to-all(bf16[4,16,128]{2,1,0:T(8,128)(2,1)S(1)} %fusion.12), channel_id=1, replica_groups=mesh['layer'=8,'plane'=4] {'plane'}, dimensions={0} | all-to-all | bytes 32768 | tf_op jit(solution)/shard_map/all_to_all | solution.py:90
  35.0 0.3 fusion.54
  35.3 0.7 collective-permute-start.2
  36.0 0.4 fusion.13
  36.3 6.2 %all_to_all.36 = bf16[4,16,128]{2,1,0:T(8,128)(2,1)S(1)} all-to-all(bf16[4,16,128]{2,1,0:T(8,128)(2,1)S(1)} %fusion.13), channel_id=1, replica_groups=mesh['layer'=8,'plane'=4] {'plane'}, dimensions={0} | all-to-all | bytes 32768 | tf_op jit(solution)/shard_map/all_to_all | solution.py:90
  42.6 0.3 fusion.55
  42.8 0.7 collective-permute-start.3
  43.5 0.4 fusion.14
  43.9 6.2 %all_to_all.37 = bf16[4,16,128]{2,1,0:T(8,128)(2,1)S(1)} all-to-all(bf16[4,16,128]{2,1,0:T(8,128)(2,1)S(1)} %fusion.14), channel_id=1, replica_groups=mesh['layer'=8,'plane'=4] {'plane'}, dimensions={0} | all-to-all | bytes 32768 | tf_op jit(solution)/shard_map/all_to_all | solution.py:90
  50.1 0.3 fusion.56
  50.3 0.7 collective-permute-start.4
  51.0 0.4 fusion.15
  51.4 6.2 %all_to_all.38 = bf16[4,16,128]{2,1,0:T(8,128)(2,1)S(1)} all-to-all(bf16[4,16,128]{2,1,0:T(8,128)(2,1)S(1)} %fusion.15), channel_id=1, replica_groups=mesh['layer'=8,'plane'=4] {'plane'}, dimensions={0} | all-to-all | bytes 32768 | tf_op jit(solution)/shard_map/all_to_all | solution.py:90
  57.6 0.3 fusion.57
  57.8 0.7 collective-permute-start.5
  58.5 0.4 fusion.16
  58.9 6.2 %all_to_all.39 = bf16[4,16,128]{2,1,0:T(8,128)(2,1)S(1)} all-to-all(bf16[4,16,128]{2,1,0:T(8,128)(2,1)S(1)} %fusion.16), channel_id=1, replica_groups=mesh['layer'=8,'plane'=4] {'plane'}, dimensions={0} | all-to-all | bytes 32768 | tf_op jit(solution)/shard_map/all_to_all | solution.py:90
  65.1 0.3 fusion.58
  65.3 1.3 %collective-permute-start.6 = (bf16[16,1024]{1,0:T(8,128)(2,1)S(1)}, bf16[16,1024]{1,0:T(8,128)(2,1)S(1)}, u32[]{:S(2)}, u32[]{:S(2)}) collective-permute-start(bf16[16,1024]{1,0:T(8,128)(2,1)S(1)} %get-tuple-element.21), channel_id=1, source_target_pairs={{24,28},{4,0},{25,29},{5,1},{26,30},{6,2},{27,31},{7,3}} | collective-permute-start | bytes 98312 | tf_op jit(solution)/shard_map/ppermute | solution.py:88
  66.6 23.5 %collective-permute-done.6 = bf16[16,1024]{1,0:T(8,128)(2,1)S(1)} collective-permute-done((bf16[16,1024]{1,0:T(8,128)(2,1)S(1)}, bf16[16,1024]{1,0:T(8,128)(2,1)S(1)}, u32[]{:S(2)}, u32[]{:S(2)}) %collective-permute-start.6) | collective-permute-done | bytes 32800 | tf_op jit(solution)/shard_map/ppermute | solution.py:88
  90.2 1.0 %fusion.17 = bf16[4,16,128]{2,1,0:T(8,128)(2,1)} fusion(bf16[1,4,128,1024]{3,2,1,0:T(8,128)(2,1)S(1)} %get-tuple-element.6, bf16[16,1024]{1,0:T(8,128)(2,1)S(1)} %collective-permute-done.6), kind=kOutput, calls=%fused_computation.31 | convolution fusion | flops 16785408 | bytes 1097728 | tf_op jit(solution)/shard_map/ikt,st->isk/dot_general | solution.py:41
  91.2 3.3 %all-to-all-start.6 = ((bf16[4,16,128]{2,1,0:T(8,128)(2,1)}), bf16[4,16,128]{2,1,0:T(8,128)(2,1)S(1)}, u32[]{:S(2)}, u32[]{:S(2)}) async-start(bf16[4,16,128]{2,1,0:T(8,128)(2,1)} %fusion.17), calls=%async_computation.6 | async-start | bytes 32768 | tf_op jit(solution)/shard_map/all_to_all | solution.py:90
  94.5 3.8 %all-to-all-done.6 = bf16[4,16,128]{2,1,0:T(8,128)(2,1)S(1)} async-done(((bf16[4,16,128]{2,1,0:T(8,128)(2,1)}), bf16[4,16,128]{2,1,0:T(8,128)(2,1)S(1)}, u32[]{:S(2)}, u32[]{:S(2)}) %all-to-all-start.6) | async-done | bytes 16416 | tf_op jit(solution)/shard_map/all_to_all | solution.py:90
  98.3 0.9 fusion.4
  (11 shorter events, 0.0 us)
Async XLA Ops:
  0.0 1.0 %copy-start = (f32[1,8,128,128]{3,2,1,0:T(8,128)S(1)}, f32[1,8,128,128]{3,2,1,0:T(8,128)}, u32[]{:S(2)}) copy-start(f32[1,8,128,128]{3,2,1,0:T(8,128)} %param.9) | copy-start | bytes 1572868
  1.0 0.8 copy-start.1
  10.9 8.0 %collective-permute-start = (bf16[16,1024]{1,0:T(8,128)(2,1)S(1)}, bf16[16,1024]{1,0:T(8,128)(2,1)S(1)}, u32[]{:S(2)}, u32[]{:S(2)}) collective-permute-start(bf16[16,1024]{1,0:T(8,128)(2,1)S(1)} %convert_element_type.67), channel_id=1, source_target_pairs={{0,4},{28,24},{1,5},{29,25},{2,6},{30,26},{3,7},{31,27}} | collective-permute-start | bytes 98312 | tf_op jit(solution)/shard_map/ppermute | solution.py:88
  15.8 1.9 %copy-start.4 = (bf16[1,4,128,1024]{3,2,1,0:T(8,128)(2,1)S(1)}, bf16[1,4,128,1024]{3,2,1,0:T(8,128)(2,1)}, u32[]{:S(2)}) copy-start(bf16[1,4,128,1024]{3,2,1,0:T(8,128)(2,1)} %param.10) | copy-start | bytes 3145732
  15.8 2.2 %copy-start.5 = (bf16[1,4,128,1024]{3,2,1,0:T(8,128)(2,1)S(1)}, bf16[1,4,128,1024]{3,2,1,0:T(8,128)(2,1)}, u32[]{:S(2)}) copy-start(bf16[1,4,128,1024]{3,2,1,0:T(8,128)(2,1)} %param.12) | copy-start | bytes 3145732
  18.0 0.7 copy-start.7
  18.1 1.0 %copy-start.2 = (bf16[1,4,128,1024]{3,2,1,0:T(8,128)(2,1)}, bf16[1,4,128,1024]{3,2,1,0:T(8,128)(2,1)S(1)}, u32[]{:S(2)}) copy-start(bf16[1,4,128,1024]{3,2,1,0:T(8,128)(2,1)S(1)} %get-tuple-element.5) | copy-start | bytes 3145732
  18.1 0.7 copy-start.6
  20.1 7.1 %all-to-all-start = ((bf16[4,16,128]{2,1,0:T(8,128)(2,1)}), bf16[4,16,128]{2,1,0:T(8,128)(2,1)S(1)}, u32[]{:S(2)}, u32[]{:S(2)}) async-start(bf16[4,16,128]{2,1,0:T(8,128)(2,1)} %fusion.11), calls=%async_computation | async-start | bytes 32768 | tf_op jit(solution)/shard_map/all_to_all | solution.py:90
  27.2 1.2 %copy-start.3 = (bf16[1,4,128,1024]{3,2,1,0:T(8,128)(2,1)S(1)}, bf16[1,4,128,1024]{3,2,1,0:T(8,128)(2,1)}, u32[]{:S(2)}) copy-start(bf16[1,4,128,1024]{3,2,1,0:T(8,128)(2,1)} %copy-done.2) | copy-start | bytes 3145732
  27.5 0.8 collective-permute-start.1
  35.3 0.7 collective-permute-start.2
  42.8 0.7 collective-permute-start.3
  50.3 0.7 collective-permute-start.4
  57.8 0.7 collective-permute-start.5
  65.3 24.8 %collective-permute-start.6 = (bf16[16,1024]{1,0:T(8,128)(2,1)S(1)}, bf16[16,1024]{1,0:T(8,128)(2,1)S(1)}, u32[]{:S(2)}, u32[]{:S(2)}) collective-permute-start(bf16[16,1024]{1,0:T(8,128)(2,1)S(1)} %get-tuple-element.21), channel_id=1, source_target_pairs={{24,28},{4,0},{25,29},{5,1},{26,30},{6,2},{27,31},{7,3}} | collective-permute-start | bytes 98312 | tf_op jit(solution)/shard_map/ppermute | solution.py:88
  91.2 7.1 %all-to-all-start.6 = ((bf16[4,16,128]{2,1,0:T(8,128)(2,1)}), bf16[4,16,128]{2,1,0:T(8,128)(2,1)S(1)}, u32[]{:S(2)}, u32[]{:S(2)}) async-start(bf16[4,16,128]{2,1,0:T(8,128)(2,1)} %fusion.17), calls=%async_computation.6 | async-start | bytes 32768 | tf_op jit(solution)/shard_map/all_to_all | solution.py:90
